TPU v7x, 32 devices: a whole 2x2x4 slice. The times are simulated.
32 devices in a mesh: groups: 2 (over x), blk: 4 (over y, core), col: 4 (over z).
Axes of the slice: x: 2, y: 2, z: 4, core: 2. Of those that a mesh axis runs over, the one named last changes fastest.
Arguments:
- pair_block: bfloat16 [4096, 16384], P(('groups', 'blk'), 'col'), parts along dimension 0, may hold values from -1.5 to 1.5
- occ_energy: float32 [2], P('groups'), parts along dimension 0, may hold values from -1.5 to -0.3
- virt_energy: float32 [4096], P('groups'), parts along dimension 0, may hold values from 0.2 to 3
- frequency: float32 [2], P('groups'), parts along dimension 0, may hold values from 0.2 to 2
Outputs:
- dielectric: float32 [32768, 16384], P(('groups', 'col'), 'blk'), parts along dimension 0
There are 2 independent parts, one for each index of `groups`. A program takes and returns all parts, laid end to end along the dimension named above; each array names one. Nothing has to cross between parts.
All inputs are finite; a program needn't handle non-finite values.
Results may differ from a plain program's by a relative error of at most 0.0027.
Values may be sent and summed in bfloat16 or wider, within the bound.
No kernel may reach another device: no remote copies, remote signals or barrier semaphores. Data moves between devices by JAX's collectives and lax.ppermute only.
A program may use at most 192 MiB of HBM per device.

v0:
```python
import jax
import jax.numpy as jnp
from jax import lax
from jax.sharding import PartitionSpec as P


def pair_weights(occ_energy, virt_energy, frequency):
    gap = (virt_energy[None, :] - occ_energy[:, None]).reshape(-1)
    return 2.0 * gap / (gap * gap + frequency[0] * frequency[0])


def shards(pair_block, occ_energy, virt_energy, frequency):
    weights = pair_weights(occ_energy, virt_energy, frequency)
    row_full = lax.all_gather(pair_block, "col", axis=1, tiled=True)
    column_slab = lax.all_to_all(row_full, "blk", split_axis=1, concat_axis=0, tiled=True)
    scaled = (
        lax.all_gather(pair_block, "blk", axis=0, tiled=True).astype(jnp.float32) * weights[:, None]
    ).astype(jnp.bfloat16)
    return lax.dot_general(
        scaled, column_slab, (((0,), (0,)), ((), ())), preferred_element_type=jnp.float32
    )


def solution(mesh):
    return jax.shard_map(
        shards,
        mesh=mesh,
        in_specs=(P(("groups", "blk"), "col"), P("groups"), P("groups"), P("groups")),
        out_specs=P(("groups", "col"), "blk"),
        check_vma=False,
    )
```

profile of v0, /device:TPU:0, one launch (start us, length us, event | category | flops | bytes accessed | tf_op | source)
XLA Modules:
  0.0 691.5 jit_solution(8358652491445676149)
XLA Ops:
  6.5 0.0 all-gather.5.cloned.1.call-start
  6.5 6.4 copy.5
  12.9 0.0 all-gather.5.cloned.1.call-update
  13.0 0.0 all-gather.3.cloned.1.call-start
  13.0 0.7 all-gather.3.cloned.1.call-update
  13.7 288.9 %all-gather.5.cloned.1.call-done = bf16[512,16384]{0,1:T(8,128)(2,1)} async-done(((bf16[512,4096]{0,1:T(8,128)(2,1)}), bf16[512,16384]{0,1:T(8,128)(2,1)}) %all-gather.5.cloned.1.call-update) | async-done | bytes 16777232 | tf_op jit(solution)/shard_map/all_gather | solution.py:14
  302.6 0.0 copy-start
  302.6 7.3 %all-to-all-start = ((bf16[512,4,4096]{0,2,1:T(8,128)(2,1)}), bf16[512,4,4096]{0,2,1:T(8,128)(2,1)}, u32[]{:S(2)}, u32[]{:S(2)}) async-start(bf16[512,4,4096]{0,2,1:T(8,128)(2,1)} %bitcast.8), calls=%async_computation | async-start | bytes 33554432 | tf_op jit(solution)/shard_map/all_to_all | solution.py:15
  311.2 0.0 copy-done
  311.2 271.6 %all-to-all-done = bf16[512,4,4096]{0,2,1:T(8,128)(2,1)} async-done(((bf16[512,4,4096]{0,2,1:T(8,128)(2,1)}), bf16[512,4,4096]{0,2,1:T(8,128)(2,1)}, u32[]{:S(2)}, u32[]{:S(2)}) %all-to-all-start) | async-done | bytes 16777248 | tf_op jit(solution)/shard_map/all_to_all | solution.py:15
  582.8 20.7 %copy.6 = bf16[4,512,4096]{2,1,0:T(8,128)(2,1)} copy(bf16[4,512,4096]{1,2,0:T(8,128)(2,1)} %bitcast.3) | data formatting | bytes 33554432 | tf_op jit(solution)/shard_map/all_to_all | solution.py:15
  603.5 0.0 all-gather.3.cloned.1.call-done
  603.5 81.2 %fusion = f32[4096,4096]{1,0:T(8,128)} fusion(bf16[2048,4096]{1,0:T(8,128)(2,1)} %bitcast.9, bf16[2048,4096]{1,0:T(8,128)(2,1)} %all-gather.3.cloned.1.call-done, f32[2048]{0:T(1024)S(1)} %add_divide_fusion), kind=kOutput, calls=%fused_computation.1 | convolution fusion | flops 68744642560 | bytes 100671488 | tf_op jit(solution)/shard_map/dot_general | solution.py:19
  (1 shorter events, 0.0 us)
Async XLA Ops:
  6.5 296.1 %all-gather.5.cloned.1.call-start = ((), (), s32[]{:S(2)}) async-start(), calls=%async_computation.2 | async-start | bytes 20971520 | tf_op jit(solution)/shard_map/all_gather | solution.py:14
  13.0 590.5 %all-gather.3.cloned.1.call-start = ((), (), s32[]{:S(2)}) async-start(), calls=%async_computation.1 | async-start | bytes 20971520 | tf_op jit(solution)/shard_map/all_gather | solution.py:17
  302.6 8.6 %copy-start = (f32[2048]{0:T(1024)S(1)}, f32[2048]{0:T(1024)}, u32[]{:S(2)}) copy-start(f32[2048]{0:T(1024)} %param.6) | copy-start | bytes 24580
  302.6 280.2 %all-to-all-start = ((bf16[512,4,4096]{0,2,1:T(8,128)(2,1)}), bf16[512,4,4096]{0,2,1:T(8,128)(2,1)}, u32[]{:S(2)}, u32[]{:S(2)}) async-start(bf16[512,4,4096]{0,2,1:T(8,128)(2,1)} %bitcast.8), calls=%async_computation | async-start | bytes 33554432 | tf_op jit(solution)/shard_map/all_to_all | solution.py:15
Sparse Core Ops, SparseCore 0:
  13.1 289.4 all-gather.4
  304.2 194.0 all-gather.2
where the time goes:
time: 692 us; the launch traced here: 691 us
  waiting for transfers between devices  561 us (81%)
  matrix products  81.2 us (12%)
  local copies, waits for them, and re-layouts  27.1 us (4%)
  between operations  14.7 us (2%)
  starting transfers between devices  7.3 us (1%)
    all_gather x1, waiting for transfers between devices, shards(): row_full = lax.all_gather(pair_block, 'col', axis=1, tiled=True)  289 us
    all_to_all x1, waiting for transfers between devices, shards(): lax.all_to_all(row_full, 'blk', split_axis=1, concat_axis=0, tiled=True)  272 us
    dot_general x1, matrix products, shards(): lax.dot_general(scaled, column_slab, (((0,), (0,)), ((), ())), preferred_...  81.2 us
    all_to_all x1, local copies, waits for them, and re-layouts, shards(): lax.all_to_all(row_full, 'blk', split_axis=1, concat_axis=0, tiled=True)  20.7 us
  transfers between devices with their start and end apart: 3, of which 2 were waited for; matrix products, arithmetic and copies ran while one was open for 3% of the time, Pallas kernels for 0%

commit v1 on v0

--- a/solution.py
+++ b/solution.py
@@ -11,7 +11,12 @@
 
 def shards(pair_block, occ_energy, virt_energy, frequency):
     weights = pair_weights(occ_energy, virt_energy, frequency)
-    row_full = lax.all_gather(pair_block, "col", axis=1, tiled=True)
+    ring = [pair_block]
+    for hop in range(3):
+        ring.append(lax.ppermute(ring[-1], "col", [(dev, (dev + 1) % 4) for dev in range(4)]))
+    row_full = jnp.roll(
+        jnp.concatenate(ring[::-1], axis=1), (lax.axis_index("col") + 1) * ring[0].shape[1], axis=1
+    )
     column_slab = lax.all_to_all(row_full, "blk", split_axis=1, concat_axis=0, tiled=True)
     scaled = (
         lax.all_gather(pair_block, "blk", axis=0, tiled=True).astype(jnp.float32) * weights[:, None]

time: 692 us -> 644 us (0.931)
  waiting for transfers between devices: 561 us -> 461 us
  local copies, waits for them, and re-layouts: 27.1 us -> 75.3 us
    all_gather x1 -> x0, waiting for transfers between devices: 289 us -> none  [shards(): row_full = lax.all_gather(pair_block, 'col', axis=1, tiled=True)]
    ppermute x0 -> x3, waiting for transfers between devices: none -> 280 us  [shards(): lax.ppermute(ring[-1], 'col', [(dev, (dev + 1) % 4) for dev in range(4)])]
    all_to_all x1, waiting for transfers between devices: 272 us -> 182 us  [shards(): lax.all_to_all(row_full, 'blk', split_axis=1, concat_axis=0, tiled=True)]
    unnamed x3 -> x12, local copies, waits for them, and re-layouts: 6.4 us -> 37.8 us
    dynamic_slice x0 -> x1, local copies, waits for them, and re-layouts: none -> 13.7 us  [shards(): jnp.roll(jnp.concatenate(ring[::-1], axis=1), (lax.axis_index('col') + 1)...]
  transfers between devices with their start and end apart: 3 -> 5, of which waited for: 2 -> 4; matrix products, arithmetic and copies ran while one was open for 3% -> 11% of each run, Pallas kernels for 0% -> 0%
where the time goes in v1:
time: 644 us; the launch traced here: 643 us
  waiting for transfers between devices  461 us (72%)
  matrix products  81.1 us (13%)
  local copies, waits for them, and re-layouts  75.3 us (12%)
  between operations  14.7 us (2%)
  starting transfers between devices  10.2 us (2%)
    ppermute x3, waiting for transfers between devices, shards(): lax.ppermute(ring[-1], 'col', [(dev, (dev + 1) % 4) for dev in range(4)])  280 us
    all_to_all x1, waiting for transfers between devices, shards(): lax.all_to_all(row_full, 'blk', split_axis=1, concat_axis=0, tiled=True)  182 us
    dot_general x1, matrix products, shards(): lax.dot_general(scaled, column_slab, (((0,), (0,)), ((), ())), preferred_...  81.1 us
    unnamed x12, local copies, waits for them, and re-layouts  37.8 us
    all_to_all x1, local copies, waits for them, and re-layouts, shards(): lax.all_to_all(row_full, 'blk', split_axis=1, concat_axis=0, tiled=True)  21.5 us
    dynamic_slice x1, local copies, waits for them, and re-layouts, shards(): jnp.roll(jnp.concatenate(ring[::-1], axis=1), (lax.axis_index('col') + 1)...  13.7 us
  transfers between devices with their start and end apart: 5, of which 4 were waited for; matrix products, arithmetic and copies ran while one was open for 11% of the time, Pallas kernels for 0%

profile of v1, /device:TPU:0, one launch (start us, length us, event | category | flops | bytes accessed | tf_op | source)
XLA Modules:
  0.0 642.6 jit_solution(11457344198630002938)
XLA Ops:
  6.5 0.0 all-gather.2.cloned.1.call-start
  6.5 6.5 %copy.5 = bf16[512,4096]{0,1:T(8,128)(2,1)} copy(bf16[512,4096]{1,0:T(8,128)(2,1)} %param.4) | data formatting | bytes 8388608 | tf_op args[0]
  13.0 3.1 collective-permute-start
  16.1 92.9 %collective-permute-done = bf16[512,4096]{0,1:T(8,128)(2,1)} collective-permute-done((bf16[512,4096]{0,1:T(8,128)(2,1)}, bf16[512,4096]{0,1:T(8,128)(2,1)}, u32[]{:S(2)}, u32[]{:S(2)}) %collective-permute-start) | collective-permute-done | bytes 4194336 | tf_op jit(solution)/shard_map/ppermute | solution.py:16
  109.0 0.0 collective-permute-start.1
  109.0 0.0 all-gather.2.cloned.1.call-update
  109.0 93.8 %collective-permute-done.1 = bf16[512,4096]{0,1:T(8,128)(2,1)} collective-permute-done((bf16[512,4096]{0,1:T(8,128)(2,1)}, bf16[512,4096]{0,1:T(8,128)(2,1)}, u32[]{:S(2)}, u32[]{:S(2)}) %collective-permute-start.1) | collective-permute-done | bytes 4194336 | tf_op jit(solution)/shard_map/ppermute | solution.py:16
  202.8 0.0 collective-permute-start.2
  202.8 0.0 copy-start
  202.8 93.0 %collective-permute-done.2 = bf16[512,4096]{0,1:T(8,128)(2,1)} collective-permute-done((bf16[512,4096]{0,1:T(8,128)(2,1)}, bf16[512,4096]{0,1:T(8,128)(2,1)}, u32[]{:S(2)}, u32[]{:S(2)}) %collective-permute-start.2) | collective-permute-done | bytes 4194336 | tf_op jit(solution)/shard_map/ppermute | solution.py:16
  295.8 4.5 constant_dynamic-update-slice_fusion.7
  300.3 4.5 constant_dynamic-update-slice_fusion.6
  304.8 4.5 constant_dynamic-update-slice_fusion.5
  309.2 4.5 constant_dynamic-update-slice_fusion.4
  313.7 4.5 constant_dynamic-update-slice_fusion.3
  318.2 4.5 constant_dynamic-update-slice_fusion.2
  322.6 4.5 constant_dynamic-update-slice_fusion.1
  327.1 0.0 copy-done
  327.1 2.3 constant_dynamic-update-slice_fusion
  329.4 0.0 copy-start.1
  329.4 13.7 %constant_dynamic-slice_fusion = bf16[512,16384]{0,1:T(8,128)(2,1)} fusion(bf16[512,32768]{0,1:T(8,128)(2,1)} %constant_dynamic-update-slice_fusion, s32[]{:T(128)S(6)} %select_n.14), kind=kLoop, calls=%fused_computation.12 | loop fusion | bytes 33554436 | tf_op jit(solution)/shard_map/jit(_roll_dynamic)/dynamic_slice | solution.py:17
  343.1 7.2 %all-to-all-start = ((bf16[512,4,4096]{0,2,1:T(8,128)(2,1)}), bf16[512,4,4096]{0,2,1:T(8,128)(2,1)}, u32[]{:S(2)}, u32[]{:S(2)}) async-start(bf16[512,4,4096]{0,2,1:T(8,128)(2,1)} %bitcast.8), calls=%async_computation | async-start | bytes 33554432 | tf_op jit(solution)/shard_map/all_to_all | solution.py:20
  351.6 0.0 copy-done.1
  351.6 181.5 %all-to-all-done = bf16[512,4,4096]{0,2,1:T(8,128)(2,1)} async-done(((bf16[512,4,4096]{0,2,1:T(8,128)(2,1)}), bf16[512,4,4096]{0,2,1:T(8,128)(2,1)}, u32[]{:S(2)}, u32[]{:S(2)}) %all-to-all-start) | async-done | bytes 16777248 | tf_op jit(solution)/shard_map/all_to_all | solution.py:20
  533.1 21.5 %copy.8 = bf16[4,512,4096]{2,1,0:T(8,128)(2,1)} copy(bf16[4,512,4096]{1,2,0:T(8,128)(2,1)} %bitcast.3) | data formatting | bytes 33554432 | tf_op jit(solution)/shard_map/all_to_all | solution.py:20
  554.6 0.0 all-gather.2.cloned.1.call-done
  554.6 81.1 %fusion = f32[4096,4096]{1,0:T(8,128)} fusion(bf16[2048,4096]{1,0:T(8,128)(2,1)} %bitcast.9, bf16[2048,4096]{1,0:T(8,128)(2,1)} %all-gather.2.cloned.1.call-done, f32[2048]{0:T(1024)S(1)} %add_divide_fusion), kind=kOutput, calls=%fused_computation.1 | convolution fusion | flops 68744642560 | bytes 100671488 | tf_op jit(solution)/shard_map/dot_general | solution.py:24
  (1 shorter events, 0.0 us)
Async XLA Ops:
  6.5 548.1 %all-gather.2.cloned.1.call-start = ((), (), s32[]{:S(2)}) async-start(), calls=%async_computation.1 | async-start | bytes 20971520 | tf_op jit(solution)/shard_map/all_gather | solution.py:22
  13.0 96.0 %collective-permute-start = (bf16[512,4096]{0,1:T(8,128)(2,1)}, bf16[512,4096]{0,1:T(8,128)(2,1)}, u32[]{:S(2)}, u32[]{:S(2)}) collective-permute-start(bf16[512,4096]{0,1:T(8,128)(2,1)} %copy.5), channel_id=1, source_target_pairs={{0,1},{1,2},{2,3},{3,0},{4,5},{5,6},{6,7},{7,4},{8,9},{9,10},{10,1... | collective-permute-start | bytes 12582920 | tf_op jit(solution)/shard_map/ppermute | solution.py:16
  109.0 93.8 %collective-permute-start.1 = (bf16[512,4096]{0,1:T(8,128)(2,1)}, bf16[512,4096]{0,1:T(8,128)(2,1)}, u32[]{:S(2)}, u32[]{:S(2)}) collective-permute-start(bf16[512,4096]{0,1:T(8,128)(2,1)} %collective-permute-done), channel_id=1, source_target_pairs={{0,1},{1,2},{2,3},{3,0},{4,5},{5,6},{6,7},{7,4},{8,9},{9,10},{10,1... | collective-permute-start | bytes 12582920 | tf_op jit(solution)/shard_map/ppermute | solution.py:16
  202.8 93.0 %collective-permute-start.2 = (bf16[512,4096]{0,1:T(8,128)(2,1)}, bf16[512,4096]{0,1:T(8,128)(2,1)}, u32[]{:S(2)}, u32[]{:S(2)}) collective-permute-start(bf16[512,4096]{0,1:T(8,128)(2,1)} %collective-permute-done.1), channel_id=1, source_target_pairs={{0,1},{1,2},{2,3},{3,0},{4,5},{5,6},{6,7},{7,4},{8,9},{9,10},{10,1... | collective-permute-start | bytes 12582920 | tf_op jit(solution)/shard_map/ppermute | solution.py:16
  202.8 124.3 %copy-start = (bf16[512,4096]{0,1:T(8,128)(2,1)S(1)}, bf16[512,4096]{0,1:T(8,128)(2,1)}, u32[]{:S(2)}) copy-start(bf16[512,4096]{0,1:T(8,128)(2,1)} %copy.5) | copy-start | bytes 12582916
  329.4 22.2 %copy-start.1 = (f32[2048]{0:T(1024)S(1)}, f32[2048]{0:T(1024)}, u32[]{:S(2)}) copy-start(f32[2048]{0:T(1024)} %param.6) | copy-start | bytes 24580
  343.1 190.0 %all-to-all-start = ((bf16[512,4,4096]{0,2,1:T(8,128)(2,1)}), bf16[512,4,4096]{0,2,1:T(8,128)(2,1)}, u32[]{:S(2)}, u32[]{:S(2)}) async-start(bf16[512,4,4096]{0,2,1:T(8,128)(2,1)} %bitcast.8), calls=%async_computation | async-start | bytes 33554432 | tf_op jit(solution)/shard_map/all_to_all | solution.py:20
Sparse Core Ops, SparseCore 0:
  109.1 107.3 all-gather.1
